TPU v7x, 32 devices: a whole 2x2x4 slice. The times are simulated.
32 devices in a mesh: groups: 2 (over y), grid: 16 (over z, x, core).
Axes of the slice: x: 2, y: 2, z: 4, core: 2. Of those that a mesh axis runs over, the one named last changes fastest.
Arguments:
- start_field: float32 [32, 1024, 128], P(('groups', 'grid')), parts along dimension 0, may hold values from -6 to 6
- col_speed: float32 [1024], replicated, may hold values from 0.5 to 2
- row_speed: float32 [32], replicated, may hold values from 0.5 to 2
- levels: int32 [32], P('groups'), parts along dimension 0, may hold values from 2 to 5, as said below
- coeffs: int32 [32], P('groups'), parts along dimension 0, may hold values from 1 to 3
- assign_first: int32 [32], P('groups'), parts along dimension 0, may hold values from 0 to 15, each once
- assign_second: int32 [32], P('groups'), parts along dimension 0, may hold values from 0 to 15, each once
- owner_of: int32 [32], P('groups'), parts along dimension 0, may hold values from 0 to 15, each once
Outputs:
- combined: float32 [2048, 1280], P(('groups', 'grid')), parts along dimension 0
- final_field: float32 [32, 1024, 128], P(('groups', 'grid')), parts along dimension 0
There are 2 independent parts, one for each index of `groups`. A program takes and returns all parts, laid end to end along the dimension named above; an argument that names none is the same for every part. Nothing has to cross between parts.
Inputs may be any that keep to these rules, and one draw needn't show every extreme that they name: `levels`: every run of 4 consecutive grids starting at a multiple of 4 holds each first level from 2 to 5 exactly once.
All inputs are finite; a program needn't handle non-finite values.
Results may differ from a plain program's by a relative error of at most 0.0003.
Values sent between devices are 32-bit elements; how exact they have to be, the bound alone decides.
No kernel may reach another device: no remote copies, remote signals or barrier semaphores. Data moves between devices by JAX's collectives and lax.ppermute only.
A program may use at most 64 MiB of HBM per device.

v0:
```python
import jax
import jax.numpy as jnp
import numpy as np
from jax import lax
from jax.sharding import PartitionSpec as P

LMIN = 2
NLEV = 4
CLEV = 5
STEPS = 2


time_step = 0.02
diffusivity = 0.0024
highest = lax.Precision.HIGHEST


def hier_line(line_level):
    points = 2**line_level
    matrix = np.zeros((points, points))
    matrix[0, 0] = 1.0
    for tier_rank in range(1, line_level + 1):
        stride = 2 ** (line_level - tier_rank)
        for entry_at in range(2 ** (tier_rank - 1), 2**tier_rank):
            node_at = (2 * (entry_at - 2 ** (tier_rank - 1)) + 1) * stride
            matrix[entry_at, node_at] += 1.0
            matrix[entry_at, (node_at - stride) % points] -= 0.5
            matrix[entry_at, (node_at + stride) % points] -= 0.5
    return matrix


def dehier_line(line_level):
    points = 2**line_level
    matrix = np.zeros((points, points))
    matrix[0, 0] = 1.0
    for tier_rank in range(1, line_level + 1):
        stride = 2 ** (line_level - tier_rank)
        for entry_at in range(2 ** (tier_rank - 1), 2**tier_rank):
            node_at = (2 * (entry_at - 2 ** (tier_rank - 1)) + 1) * stride
            matrix[node_at] = 0.5 * (
                matrix[(node_at - stride) % points] + matrix[(node_at + stride) % points]
            )
            matrix[node_at, entry_at] += 1.0
    return matrix


def row_tables():
    row_bits = 2 * LMIN + NLEV - 1
    starts, widths, offsets = ([], [], [])
    running = 0
    for piece_level in range(LMIN, LMIN + NLEV):
        first_row = 0 if piece_level == LMIN else 2 ** (piece_level - 1)
        breadth = 2**LMIN if piece_level == LMIN else 2 ** (piece_level - 1)
        starts.append(first_row)
        widths.append(breadth)
        offsets.append(running)
        running += breadth * 2 ** (row_bits - piece_level)
    forward, backward, embeds, places = ([], [], [], [])
    for shift_level in range(NLEV):
        first_level = LMIN + shift_level
        second_level = row_bits - first_level
        tensor = np.kron(hier_line(first_level), hier_line(second_level))
        inverse = np.kron(dehier_line(first_level), dehier_line(second_level))
        order_list, place_list = ([], [])
        for slot_index in range(shift_level + 1):
            for second in range(2**second_level):
                for first_idx in range(starts[slot_index], starts[slot_index] + widths[slot_index]):
                    order_list.append(first_idx * 2**second_level + second)
                    place_list.append(
                        offsets[slot_index]
                        + second * widths[slot_index]
                        + first_idx
                        - starts[slot_index]
                    )
        embedding = np.zeros((running, 2**row_bits))
        embedding[np.array(place_list), np.arange(2**row_bits)] = 1.0
        forward.append(tensor[order_list])
        backward.append(inverse[:, order_list])
        embeds.append(embedding)
        places.append(place_list)
    return (
        jnp.asarray(np.stack(forward), jnp.float32),
        jnp.asarray(np.stack(backward), jnp.float32),
        jnp.asarray(np.stack(embeds), jnp.float32),
        jnp.asarray(np.array(places), jnp.int32),
    )


def column_pass(values, matrix):
    side_cells = matrix.shape[0]
    cube_view = values.reshape(side_cells, side_cells, values.shape[-1])
    cube_view = jnp.einsum("ab,bjr->ajr", matrix, cube_view, precision=highest)
    cube_view = jnp.einsum("ab,jbr->jar", matrix, cube_view, precision=highest)
    return cube_view.reshape(values.shape)


def advance(values, grid_level, count, col_speed, row_speed):
    side_cells = 2**CLEV
    total_rows = values.shape[1]
    row_bits = 2 * LMIN + NLEV - 1
    other_level = row_bits - grid_level
    inner_count = jnp.left_shift(jnp.int32(1), other_level)
    inner_pos = jnp.bitwise_and(jnp.arange(total_rows, dtype=jnp.int32), inner_count - 1)
    sample_at = inner_pos * jnp.left_shift(jnp.int32(1), row_bits - LMIN - other_level)
    fine_cells = row_speed.shape[0]
    row_factor = jnp.sum(
        jnp.where(
            sample_at[:, None] == jnp.arange(fine_cells, dtype=jnp.int32)[None, :],
            row_speed[None, :],
            jnp.zeros_like(row_speed)[None, :],
        ),
        axis=1,
    )
    velocity = col_speed[:, None] * row_factor[None, :]
    refine = jnp.left_shift(jnp.int32(1), grid_level - LMIN)
    dt_sub = time_step / refine.astype(jnp.float32)
    scale_one = jnp.left_shift(jnp.int32(1), grid_level).astype(jnp.float32)
    scale_two = inner_count.astype(jnp.float32)
    coeff_side = float(4**CLEV)
    at_last = (inner_pos == inner_count - 1)[None, :]
    at_first = (inner_pos == 0)[None, :]

    def one_substep(turn_index, current):
        up_one = jnp.roll(current, -inner_count, axis=1)
        down_one = jnp.roll(current, inner_count, axis=1)
        up_two = jnp.where(
            at_last, jnp.roll(current, inner_count - 1, axis=1), jnp.roll(current, -1, axis=1)
        )
        down_two = jnp.where(
            at_first, jnp.roll(current, 1 - inner_count, axis=1), jnp.roll(current, 1, axis=1)
        )
        cube_view = current.reshape(side_cells, side_cells, total_rows)
        across = (
            jnp.roll(cube_view, 1, axis=0)
            + jnp.roll(cube_view, -1, axis=0)
            + jnp.roll(cube_view, 1, axis=1)
            + jnp.roll(cube_view, -1, axis=1)
        )
        across = across.reshape(current.shape) - 4.0 * current
        spread = (
            scale_one * scale_one * (up_one + down_one - 2.0 * current)
            + scale_two * scale_two * (up_two + down_two - 2.0 * current)
            + coeff_side * across
        )
        transport = velocity * (up_one - down_one) * (0.5 * scale_one)
        return current + dt_sub * (diffusivity * spread - transport)

    return lax.fori_loop(jnp.int32(0), refine * count, one_substep, values)


def local(start_field, col_speed, row_speed, levels, coeffs, assign_first, assign_second, owner_of):
    forward, backward, embeds, places = row_tables()
    column_hier = jnp.asarray(hier_line(CLEV), jnp.float32)
    column_back = jnp.asarray(dehier_line(CLEV), jnp.float32)
    cover = jnp.sum(embeds, axis=2)
    section_rows = embeds.shape[1]
    devices = lax.axis_size("grid")
    my_index = lax.axis_index("grid")
    grid_count = levels.shape[0]
    total_cols = start_field.shape[1]
    total_rows = start_field.shape[2]
    block_cols = total_cols // devices
    sections = devices // NLEV
    grid_ids = jnp.arange(grid_count, dtype=jnp.int32)
    section_ids = jnp.arange(sections, dtype=jnp.int32)
    level_ids = LMIN + jnp.arange(NLEV, dtype=jnp.int32)
    weights = coeffs.astype(jnp.float32)
    section_all = (grid_ids[:, None] // NLEV == section_ids[None, :]).astype(jnp.float32)
    level_all = (levels[:, None] == level_ids[None, :]).astype(jnp.float32) * weights[:, None]
    denominator = jnp.dot(
        jnp.dot(section_all.T, level_all, precision=highest), cover, precision=highest
    )

    def holders(assignment):
        return jnp.sum(
            jnp.where(assignment[None, :] == grid_ids[:, None], grid_ids[None, :], 0), axis=1
        )

    def lookup(table, wanted):
        return jnp.sum(
            jnp.where(
                wanted[:, None] == grid_ids[None, :], table[None, :], jnp.zeros_like(table)[None, :]
            ),
            axis=1,
        )

    def pick_entry(table, wanted):
        return jnp.sum(jnp.where(grid_ids == wanted, table, jnp.zeros_like(table)))

    owner_inv = holders(owner_of)
    first_grids = holders(assign_first)
    second_grids = holders(assign_second)
    own_first = pick_entry(first_grids, my_index)
    own_second = pick_entry(second_grids, my_index)
    level_first = pick_entry(levels, own_first)
    level_second = pick_entry(levels, own_second)
    weight_first = pick_entry(weights, own_first)
    weight_second = pick_entry(weights, own_second)

    def hierarchize(values, grid_level):
        mixed = column_pass(values, column_hier)
        return jnp.dot(mixed, forward[grid_level - LMIN].T, precision=highest)

    def dehierarchize(values, grid_level):
        mixed = jnp.dot(values, backward[grid_level - LMIN].T, precision=highest)
        return column_pass(mixed, column_back)

    def combine(surplus, my_weight, sender_grids):
        blocks = (surplus * my_weight).reshape(devices, block_cols, total_rows)
        outgoing = jnp.take(blocks, owner_inv, axis=0)
        source_levels = lookup(levels, sender_grids)
        section_hot = (sender_grids[:, None] // NLEV == section_ids[None, :]).astype(jnp.float32)
        incoming = lax.all_to_all(outgoing, "grid", split_axis=0, concat_axis=0, tiled=True)
        total = jnp.zeros((block_cols, sections, section_rows), jnp.float32)
        for shift_level in range(NLEV):
            level_mask = (
                section_hot * (source_levels == LMIN + shift_level).astype(jnp.float32)[:, None]
            )
            grouped = jnp.einsum("skr,sp->kpr", incoming, level_mask, precision=highest)
            total = total + jnp.einsum(
                "kpr,cr->kpc", grouped, embeds[shift_level], precision=highest
            )
        return total / denominator[None, :, :]

    def give_back(section_values, dest_grids, my_level):
        dest_sections = dest_grids // NLEV
        picked = jnp.take(section_values, dest_sections, axis=1)
        incoming = lax.all_to_all(picked, "grid", split_axis=1, concat_axis=0, tiled=True)
        arranged = incoming.reshape(devices, block_cols, section_rows)
        ordered = jnp.take(arranged, owner_of, axis=0).reshape(total_cols, section_rows)
        return jnp.take(ordered, places[my_level - LMIN], axis=1)

    current = advance(start_field[0], level_first, STEPS, col_speed, row_speed)
    first_combined = combine(hierarchize(current, level_first), weight_first, first_grids)
    restricted = give_back(first_combined, second_grids, level_second)
    current = advance(
        dehierarchize(restricted, level_second), level_second, STEPS, col_speed, row_speed
    )
    second_combined = combine(hierarchize(current, level_second), weight_second, second_grids)
    restricted = give_back(second_combined, second_grids, level_second)
    current = advance(
        dehierarchize(restricted, level_second), level_second, 1, col_speed, row_speed
    )
    return (second_combined.reshape(block_cols, sections * section_rows), current[None])


def solution(mesh):
    placed = (
        P(("groups", "grid"), None, None),
        P(),
        P(),
        P("groups"),
        P("groups"),
        P("groups"),
        P("groups"),
        P("groups"),
    )
    return jax.shard_map(
        local,
        mesh=mesh,
        in_specs=placed,
        out_specs=(P(("groups", "grid"), None), P(("groups", "grid"), None, None)),
        check_vma=False,
    )
```

profile of v0, /device:TPU:20, one launch (start us, length us, event | category | flops | bytes accessed | tf_op | source)
XLA Modules:
  0.0 268.2 jit_solution(7163760308921973153)
XLA Ops:
  0.6 1.0 copy.170
  4.7 2.7 %fusion.160 = (s32[]{:T(128)}, s32[]{:T(128)}) fusion(s32[16]{0:T(128)} %param.33, s32[]{:T(128)} %get-tuple-element.796, s32[]{:T(128)} %get-tuple-element.793), kind=kLoop, calls=%fused_computation.274 | loop fusion | flops 94 | bytes 80 | tf_op jit(solution)/shard_map/reduce_sum | solution.py:188
  10.4 2.6 fusion.161
  13.8 5.3 %while.42 = (s32[]{:T(128)}, f32[1024,128]{1,0:T(8,128)S(1)}, s32[]{:T(128)}, f32[]{:T(128)}, f32[]{:T(128)}, /*index=5*/s32[]{:T(128)}, s32[]{:T(128)}, f32[]{:...) while((s32[]{:T(128)}, f32[1024,128]{1,0:T(8,128)S(1)}, ...), condition=%wide.region_8.10_spmd.clone.clone, body=%wide.region_7.9_spmd.clone.clone.sunk | while | flops 4063678 | bytes 15750993 | solution.py:148
  20.9 2.0 convolution_multiply_fusion.1
  24.4 41.7 %all-to-all-start = ((f32[16,64,128]{2,1,0:T(8,128)}), f32[16,64,128]{2,1,0:T(8,128)S(1)}, u32[]{:S(2)}, u32[]{:S(2)}) async-start(f32[16,64,128]{2,1,0:T(8,128)} %broadcast_select_fusion.3), calls=%async_computation | async-start | bytes 1048576 | tf_op jit(solution)/shard_map/all_to_all | solution.py:213
  67.3 12.7 %all-to-all-done = f32[16,64,128]{2,1,0:T(8,128)S(1)} async-done(((f32[16,64,128]{2,1,0:T(8,128)}), f32[16,64,128]{2,1,0:T(8,128)S(1)}, u32[]{:S(2)}, u32[]{:S(2)}) %all-to-all-start) | async-done | bytes 524320 | tf_op jit(solution)/shard_map/all_to_all | solution.py:213
  85.2 1.4 select_bitcast_fusion.1
  86.6 4.7 %all-to-all-start.1 = ((f32[64,16,320]{2,0,1:T(8,128)}), f32[64,16,320]{2,0,1:T(8,128)S(1)}, u32[]{:S(2)}, u32[]{:S(2)}) async-start(f32[64,16,320]{2,0,1:T(8,128)} %select_bitcast_fusion.1), calls=%async_computation.1 | async-start | bytes 3145728 | tf_op jit(solution)/shard_map/all_to_all | solution.py:228
  94.2 33.5 %all-to-all-done.1 = f32[64,16,320]{2,0,1:T(8,128)S(1)} async-done(((f32[64,16,320]{2,0,1:T(8,128)}), f32[64,16,320]{2,0,1:T(8,128)S(1)}, u32[]{:S(2)}, u32[]{:S(2)}) %all-to-all-start.1) | async-done | bytes 1310752 | tf_op jit(solution)/shard_map/all_to_all | solution.py:228
  128.3 1.4 broadcast_select_fusion.1
  129.8 1.9 copy.77
  132.8 1.7 fusion.61
  136.0 34.5 %while.43 = (s32[]{:T(128)}, f32[1024,128]{1,0:T(8,128)S(1)}, s32[]{:T(128)}, f32[]{:T(128)}, f32[]{:T(128)}, /*index=5*/s32[]{:T(128)}, s32[]{:T(128)}, f32[]{:...) while((s32[]{:T(128)}, f32[1024,128]{1,0:T(8,128)S(1)}, ...), condition=%wide.region_16.22_spmd.clone.clone, body=%wide.region_15.21_spmd.clone.clone.sunk | while | flops 4063678 | bytes 15734581 | solution.py:148
  172.3 2.0 convolution_multiply_fusion
  175.7 4.7 %all-to-all-start.2 = ((f32[16,64,128]{2,1,0:T(8,128)}), f32[16,64,128]{2,1,0:T(8,128)S(1)}, u32[]{:S(2)}, u32[]{:S(2)}) async-start(f32[16,64,128]{2,1,0:T(8,128)} %broadcast_select_fusion.2), calls=%async_computation.2 | async-start | bytes 1048576 | tf_op jit(solution)/shard_map/all_to_all | solution.py:213
  180.5 13.8 %all-to-all-done.2 = f32[16,64,128]{2,1,0:T(8,128)S(1)} async-done(((f32[16,64,128]{2,1,0:T(8,128)}), f32[16,64,128]{2,1,0:T(8,128)S(1)}, u32[]{:S(2)}, u32[]{:S(2)}) %all-to-all-start.2) | async-done | bytes 524320 | tf_op jit(solution)/shard_map/all_to_all | solution.py:213
  199.5 1.4 select_bitcast_fusion
  200.9 4.6 %all-to-all-start.3 = ((f32[64,16,320]{2,0,1:T(8,128)}), f32[64,16,320]{2,0,1:T(8,128)S(1)}, u32[]{:S(2)}, u32[]{:S(2)}) async-start(f32[64,16,320]{2,0,1:T(8,128)} %select_bitcast_fusion), calls=%async_computation.3 | async-start | bytes 3145728 | tf_op jit(solution)/shard_map/all_to_all | solution.py:228
  206.7 35.1 %all-to-all-done.3 = f32[64,16,320]{2,0,1:T(8,128)S(1)} async-done(((f32[64,16,320]{2,0,1:T(8,128)}), f32[64,16,320]{2,0,1:T(8,128)S(1)}, u32[]{:S(2)}, u32[]{:S(2)}) %all-to-all-start.3) | async-done | bytes 1310752 | tf_op jit(solution)/shard_map/all_to_all | solution.py:228
  242.5 1.4 broadcast_select_fusion
  243.9 1.9 copy.92
  246.9 1.7 fusion.59
  250.2 17.2 %while.44 = (s32[]{:T(128)}, f32[1024,128]{1,0:T(8,128)S(1)}, s32[]{:T(128)}, f32[]{:T(128)}, f32[]{:T(128)}, /*index=5*/s32[]{:T(128)}, s32[]{:T(128)}, f32[]{:...) while((s32[]{:T(128)}, f32[1024,128]{1,0:T(8,128)S(1)}, ...), condition=%wide.region_19.25_spmd.clone.clone, body=%wide.region_18.24_spmd.clone.clone.sunk | while | flops 4063678 | bytes 15734581 | solution.py:148
  (399 shorter events, 83.2 us)
Async XLA Ops:
  13.8 5.3 %copy-start.9 = (f32[32,32,1]{1,0,2:T(8,128)S(1)}, f32[32,32,1]{1,0,2:T(8,128)}, u32[]{:S(2)}) copy-start(f32[32,32,1]{1,0,2:T(8,128)} %constant.249) | copy-start | bytes 12292
  22.9 43.2 %copy-start.19 = (s32[16]{0:T(128)S(1)}, s32[16]{0:T(128)}, u32[]{:S(2)}) copy-start(s32[16]{0:T(128)} %param.34) | copy-start | bytes 196
  22.9 43.3 %copy-start.13 = (s32[16]{0:T(128)S(1)}, s32[16]{0:T(128)}, u32[]{:S(2)}) copy-start(s32[16]{0:T(128)} %param.33) | copy-start | bytes 196
  22.9 44.3 %copy-start.10 = (f32[4,320]{1,0:T(4,128)S(1)}, f32[4,320]{1,0:T(4,128)}, u32[]{:S(2)}) copy-start(f32[4,320]{1,0:T(4,128)} %constant.248) | copy-start | bytes 15364
  23.5 57.1 %copy-start.3 = (f32[320,128,1]{1,0,2:T(8,128)S(1)}, f32[320,128,1]{1,0,2:T(8,128)}, u32[]{:S(2)}) copy-start(f32[320,128,1]{1,0,2:T(8,128)} %constant.251) | copy-start | bytes 491524
  24.4 57.4 %copy-start.5 = (f32[320,128,1]{1,0,2:T(8,128)S(1)}, f32[320,128,1]{1,0,2:T(8,128)}, u32[]{:S(2)}) copy-start(f32[320,128,1]{1,0,2:T(8,128)} %constant.252) | copy-start | bytes 491524
  24.4 55.6 %all-to-all-start = ((f32[16,64,128]{2,1,0:T(8,128)}), f32[16,64,128]{2,1,0:T(8,128)S(1)}, u32[]{:S(2)}, u32[]{:S(2)}) async-start(f32[16,64,128]{2,1,0:T(8,128)} %broadcast_select_fusion.3), calls=%async_computation | async-start | bytes 1048576 | tf_op jit(solution)/shard_map/all_to_all | solution.py:213
  66.2 19.0 %copy-start.15 = (pred[16]{0:T(512)(128)(4,1)}, pred[16]{0:T(512)(128)(4,1)S(1)}, u32[]{:S(2)}) copy-start(pred[16]{0:T(512)(128)(4,1)S(1)} %get-tuple-element.740) | copy-start | bytes 52
  80.7 2.3 copy-start.4
  81.8 2.3 copy-start.21
  86.6 7.5 %copy-start.20 = (s32[16]{0:T(128)S(1)}, s32[16]{0:T(128)}, u32[]{:S(2)}) copy-start(s32[16]{0:T(128)} %param.37) | copy-start | bytes 196
  86.6 41.1 %all-to-all-start.1 = ((f32[64,16,320]{2,0,1:T(8,128)}), f32[64,16,320]{2,0,1:T(8,128)S(1)}, u32[]{:S(2)}, u32[]{:S(2)}) async-start(f32[64,16,320]{2,0,1:T(8,128)} %select_bitcast_fusion.1), calls=%async_computation.1 | async-start | bytes 3145728 | tf_op jit(solution)/shard_map/all_to_all | solution.py:228
  94.1 38.3 %copy-start.11 = (pred[128]{0:T(512)(128)(4,1)}, pred[128]{0:T(512)(128)(4,1)S(1)}, u32[]{:S(2)}) copy-start(pred[128]{0:T(512)(128)(4,1)S(1)} %get-tuple-element.738) | copy-start | bytes 388
  94.2 34.2 %copy-start.17 = (pred[16]{0:T(512)(128)(4,1)}, pred[16]{0:T(512)(128)(4,1)S(1)}, u32[]{:S(2)}) copy-start(pred[16]{0:T(512)(128)(4,1)S(1)} %compare_and_fusion.2) | copy-start | bytes 52
  132.4 2.0 copy-start.7
  132.8 3.2 %copy-start.2 = (f32[1024]{0:T(1024)S(1)}, f32[1024]{0:T(1024)}, u32[]{:S(2)}) copy-start(f32[1024]{0:T(1024)} %get-tuple-element.1287) | copy-start | bytes 12292
  174.2 6.2 %copy-start.14 = (s32[16]{0:T(128)S(1)}, s32[16]{0:T(128)}, u32[]{:S(2)}) copy-start(s32[16]{0:T(128)} %get-tuple-element.652) | copy-start | bytes 196
  175.7 20.3 %copy-start.6 = (f32[320,128,1]{1,0,2:T(8,128)S(1)}, f32[320,128,1]{1,0,2:T(8,128)}, u32[]{:S(2)}) copy-start(f32[320,128,1]{1,0,2:T(8,128)} %constant.252) | copy-start | bytes 491524
  175.7 18.6 %all-to-all-start.2 = ((f32[16,64,128]{2,1,0:T(8,128)}), f32[16,64,128]{2,1,0:T(8,128)S(1)}, u32[]{:S(2)}, u32[]{:S(2)}) async-start(f32[16,64,128]{2,1,0:T(8,128)} %broadcast_select_fusion.2), calls=%async_computation.2 | async-start | bytes 1048576 | tf_op jit(solution)/shard_map/all_to_all | solution.py:213
  196.1 2.2 copy-start.22
  200.9 41.0 %all-to-all-start.3 = ((f32[64,16,320]{2,0,1:T(8,128)}), f32[64,16,320]{2,0,1:T(8,128)S(1)}, u32[]{:S(2)}, u32[]{:S(2)}) async-start(f32[64,16,320]{2,0,1:T(8,128)} %select_bitcast_fusion), calls=%async_computation.3 | async-start | bytes 3145728 | tf_op jit(solution)/shard_map/all_to_all | solution.py:228
  245.8 0.8 copy-start.12
  246.6 2.0 copy-start.8
  267.4 0.8 copy-start
  (4 other events, 2.7 us)
where the time goes:
time: 270 us; the launch traced here: 268 us
  waiting for transfers between devices  95.1 us (35%)
  starting transfers between devices  55.7 us (21%)
  other arithmetic  52 us (19%)
  local copies, waits for them, and re-layouts  31.1 us (12%)
  matrix products  23.1 us (9%)
  between operations  6.52 us (2%)
  loops' own time  4.63 us (2%)
    all_to_all x2, waiting for transfers between devices, give_back(): lax.all_to_all(picked, 'grid', split_axis=1, concat_axis=0, tiled=True)  68.6 us
    all_to_all x2, starting transfers between devices, combine(): lax.all_to_all(outgoing, 'grid', split_axis=0, concat_axis=0, tiled=True)  46.4 us
    add x26, other arithmetic, one_substep(): return current + dt_sub * (diffusivity * spread - transport)  26.8 us
    all_to_all x2, waiting for transfers between devices, combine(): lax.all_to_all(outgoing, 'grid', split_axis=0, concat_axis=0, tiled=True)  26.5 us
    slice x52, local copies, waits for them, and re-layouts, one_substep(): jnp.roll(current, 1, axis=1)  10.5 us
    all_to_all x2, starting transfers between devices, give_back(): lax.all_to_all(picked, 'grid', split_axis=1, concat_axis=0, tiled=True)  9.29 us
    add x26, other arithmetic, one_substep(): jnp.roll(cube_view, 1, axis=0) + jnp.roll(cube_view, -1, axis=0)  6.84 us
  transfers between devices with their start and end apart: 4, of which 4 were waited for; matrix products, arithmetic and copies ran while one was open for 1% of the time, Pallas kernels for 0%

commit v1 on v0

v1 whole, which is shorter than its diff:
```python
import functools

import jax
import jax.numpy as jnp
import numpy as np
from jax import lax
from jax.experimental import pallas as pl
from jax.experimental.pallas import tpu as pltpu
from jax.sharding import PartitionSpec as P

LMIN = 2
NLEV = 4
CLEV = 5
STEPS = 2

time_step = 0.02
diffusivity = 0.0024

SIDE = 2**CLEV
QUADS = SIDE // 8
ROW_BITS = 2 * LMIN + NLEV - 1
SHARED = 96
SMEM = pl.BlockSpec(memory_space=pltpu.SMEM)
VMEM = pl.BlockSpec(memory_space=pltpu.VMEM)


def hier_line(line_level):
    points = 2**line_level
    matrix = np.zeros((points, points))
    matrix[0, 0] = 1.0
    for tier_rank in range(1, line_level + 1):
        stride = 2 ** (line_level - tier_rank)
        for entry_at in range(2 ** (tier_rank - 1), 2**tier_rank):
            node_at = (2 * (entry_at - 2 ** (tier_rank - 1)) + 1) * stride
            matrix[entry_at, node_at] += 1.0
            matrix[entry_at, (node_at - stride) % points] -= 0.5
            matrix[entry_at, (node_at + stride) % points] -= 0.5
    return matrix


def dehier_line(line_level):
    points = 2**line_level
    matrix = np.zeros((points, points))
    matrix[0, 0] = 1.0
    for tier_rank in range(1, line_level + 1):
        stride = 2 ** (line_level - tier_rank)
        for entry_at in range(2 ** (tier_rank - 1), 2**tier_rank):
            node_at = (2 * (entry_at - 2 ** (tier_rank - 1)) + 1) * stride
            matrix[node_at] = 0.5 * (
                matrix[(node_at - stride) % points] + matrix[(node_at + stride) % points]
            )
            matrix[node_at, entry_at] += 1.0
    return matrix


def row_tables():
    starts = [0 if k == 0 else 2 ** (LMIN + k - 1) for k in range(NLEV)]
    widths = [2**LMIN if k == 0 else 2 ** (LMIN + k - 1) for k in range(NLEV)]
    forward, backward = ([], [])
    for shift_level in range(NLEV):
        first_level = LMIN + shift_level
        second_level = ROW_BITS - first_level
        tensor = np.kron(hier_line(first_level), hier_line(second_level))
        inverse = np.kron(dehier_line(first_level), dehier_line(second_level))
        order_list = []
        for slot_index in range(shift_level + 1):
            for second in range(2**second_level):
                for first_idx in range(starts[slot_index], starts[slot_index] + widths[slot_index]):
                    order_list.append(first_idx * 2**second_level + second)
        forward.append(tensor[order_list].T)
        backward.append(inverse[:, order_list].T)
    return (
        jnp.asarray(np.stack(forward), jnp.bfloat16),
        jnp.asarray(np.stack(backward), jnp.bfloat16),
    )


def pick(level, values):
    out = jnp.float32(values[0])
    for k in range(1, NLEV):
        out = jnp.where(level == LMIN + k, jnp.float32(values[k]), out)
    return out


def find_grid(assign_ref, me):
    def look(g, found):
        return jnp.where(assign_ref[g] == me, g, found)

    return lax.fori_loop(0, assign_ref.shape[0], look, jnp.int32(0))


def lanes():
    return lax.broadcasted_iota(jnp.int32, (8, 128), 1)


def tile(m, v):
    return pl.ds(m * SIDE + v * 8, 8)


def spread(m, v):
    return pl.ds(m * SIDE + v, 8, stride=QUADS)


def fill_speed(cs_ref, rs_ref, level, csb, speed):
    per = cs_ref.shape[1]
    for r in range(cs_ref.shape[0]):
        csb[pl.ds(r * per, per), :] = jnp.transpose(
            jnp.broadcast_to(cs_ref[pl.ds(r, 1), :], (per, per))
        )
    other = ROW_BITS - level
    inner = jnp.left_shift(jnp.int32(1), other)
    sample = jnp.bitwise_and(lanes(), inner - 1) * jnp.left_shift(jnp.int32(1), ROW_BITS - LMIN - other)
    factor = jnp.zeros((8, 128), jnp.float32)
    for k in range(rs_ref.shape[0]):
        factor = jnp.where(sample == k, rs_ref[k], factor)
    factor = factor * jnp.float32(0.5 * time_step * 2**LMIN)
    for m in range(SIDE):
        for v in range(QUADS):
            speed[tile(m, v), :] = csb[spread(m, v), :] * factor


def fill_drift(speed, level, drift):
    along = pick(level, [diffusivity * time_step * 4 ** (LMIN + k) / 2**k for k in range(NLEV)])
    for t in range(SIDE * QUADS):
        rows = pl.ds(t * 8, 8)
        one = speed[rows, :]
        drift[0, rows, :] = along - one
        drift[1, rows, :] = along + one


def advance(state, drift, level, count):
    other = ROW_BITS - level
    inner = jnp.left_shift(jnp.int32(1), other)
    refine = jnp.left_shift(jnp.int32(1), level - LMIN)
    across = [diffusivity * time_step * 4 ** (ROW_BITS - LMIN - k) / 2**k for k in range(NLEV)]
    along = [diffusivity * time_step * 4 ** (LMIN + k) / 2**k for k in range(NLEV)]
    outer = [diffusivity * time_step * 4**CLEV / 2**k for k in range(NLEV)]
    keep = [1.0 - 2.0 * across[k] - 2.0 * along[k] - 4.0 * outer[k] for k in range(NLEV)]
    coef_two = pick(level, across)
    coef_col = pick(level, outer)
    coef_own = pick(level, keep)
    shape = (SIDE, 128)
    lane = lax.broadcasted_iota(jnp.int32, shape, 1)
    place = jnp.bitwise_and(lane, inner - 1)
    at_last = place == inner - 1
    at_first = place == 0

    def one_substep(step, carry):
        now = jnp.bitwise_and(step, 1)
        later = 1 - now
        src = state.at[now]
        dst = state.at[later]

        def plane(m):
            return src[pl.ds((m % SIDE) * SIDE, SIDE), :]

        below, mid = plane(SIDE - 1), plane(0)
        for m in range(SIDE):
            above = plane(m + 1)
            rows = pl.ds(m * SIDE, SIDE)
            acc = coef_own * mid
            acc += drift[0, rows, :] * pltpu.roll(mid, 128 - inner, 1)
            acc += drift[1, rows, :] * pltpu.roll(mid, inner, 1)
            up = jnp.where(at_last, pltpu.roll(mid, inner - 1, 1), pltpu.roll(mid, 127, 1))
            down = jnp.where(at_first, pltpu.roll(mid, 129 - inner, 1), pltpu.roll(mid, 1, 1))
            acc += coef_two * (up + down)
            ahead = jnp.concatenate([mid[8:], pltpu.roll(mid[:8], 7, 0)], axis=0)
            behind = jnp.concatenate([pltpu.roll(mid[SIDE - 8 :], 1, 0), mid[: SIDE - 8]], axis=0)
            acc += coef_col * ((above + below) + (ahead + behind))
            dst[rows, :] = acc
            below, mid = mid, above
        return carry

    steps = refine * count
    lax.fori_loop(0, steps, one_substep, jnp.int32(0))
    return jnp.bitwise_and(steps, 1)


def exact_dot(values, matrix):
    high = values.astype(jnp.bfloat16)
    rest = values - high.astype(jnp.float32)
    middle = rest.astype(jnp.bfloat16)
    low = (rest - middle.astype(jnp.float32)).astype(jnp.bfloat16)
    dot = functools.partial(jnp.dot, preferred_element_type=jnp.float32)
    return dot(low, matrix) + dot(middle, matrix) + dot(high, matrix)


def pack(tiles):
    lane = lanes()
    kept = lane < SHARED
    return [jnp.where(kept, tiles[k], pltpu.roll(tiles[3], 96 - 32 * k, 1)) for k in range(3)]


def unpack(packed):
    lane = lanes()
    last = jnp.where(
        lane < 32,
        pltpu.roll(packed[0], 32, 1),
        jnp.where(lane < 64, pltpu.roll(packed[1], 64, 1), pltpu.roll(packed[2], 96, 1)),
    )
    return [packed[0], packed[1], packed[2], last]


def packed_rows(block_cols):
    return block_cols * 3 // 4 if block_cols % 32 == 0 else block_cols


def store_shared(ref, index, block_cols, group, tiles):
    if block_cols % 32 == 0:
        for k, one in enumerate(pack(tiles)):
            ref[index, pl.ds(group * 24 + k * 8, 8), :] = one
    else:
        for k, one in enumerate(tiles):
            ref[index, pl.ds(group * 32 + k * 8, 8), :] = one


def load_shared(ref, index, block_cols, group, count):
    if block_cols % 32 == 0:
        return unpack([ref[index, pl.ds(group * 24 + k * 8, 8), :] for k in range(3)])
    return [ref[index, pl.ds(group * 32 + k * 8, 8), :] for k in range(count)]


def groups_of(block_cols):
    return [(g, min(4, block_cols // 8 - 4 * g)) for g in range((block_cols + 31) // 32)]


def line_levels(bits):
    out = []
    for tier in range(1, bits + 1):
        stride = 2 ** (bits - tier)
        for entry in range(2 ** (tier - 1), 2**tier):
            out.append(((2 * (entry - 2 ** (tier - 1)) + 1) * stride, entry, stride))
    return out


def sublane_hier(x):
    sub = lax.broadcasted_iota(jnp.int32, x.shape, 0)
    fine = 0.5 * (pltpu.roll(x, 1, 0) + pltpu.roll(x, 7, 0))
    half = 0.5 * (pltpu.roll(x, 2, 0) + pltpu.roll(x, 6, 0))
    coarse = pltpu.roll(x, 4, 0)
    minus = jnp.where(
        jnp.bitwise_and(sub, 1) == 1,
        fine,
        jnp.where(jnp.bitwise_and(sub, 3) == 2, half, jnp.where(sub == 4, coarse, 0.0)),
    )
    y = x - minus
    out = y
    for entry, node in enumerate((0, 4, 2, 6, 1, 3, 5, 7)):
        if entry != node:
            out = jnp.where(sub == entry, pltpu.roll(y, (entry - node) % 8, 0), out)
    return out


def sublane_dehier(w):
    sub = lax.broadcasted_iota(jnp.int32, w.shape, 0)
    x = w
    for entry, node in enumerate((0, 4, 2, 6, 1, 3, 5, 7)):
        if entry != node:
            x = jnp.where(sub == node, pltpu.roll(w, (node - entry) % 8, 0), x)
    x = x + jnp.where(sub == 4, pltpu.roll(x, 4, 0), 0.0)
    x = x + jnp.where(jnp.bitwise_and(sub, 3) == 2, 0.5 * (pltpu.roll(x, 2, 0) + pltpu.roll(x, 6, 0)), 0.0)
    x = x + jnp.where(jnp.bitwise_and(sub, 1) == 1, 0.5 * (pltpu.roll(x, 1, 0) + pltpu.roll(x, 7, 0)), 0.0)
    return x


def column_hier(state, natural):
    def put(index, quads):
        x0, x1, x2, x3 = quads
        ahead = pltpu.roll(x0, 7, 0)
        base = index * SIDE
        natural[pl.ds(base, 8), :] = sublane_hier(x0)
        natural[pl.ds(base + 8, 8), :] = x2 - 0.5 * (x0 + ahead)
        natural[pl.ds(base + 16, 8, stride=2), :] = x1 - 0.5 * (x0 + x2)
        natural[pl.ds(base + 17, 8, stride=2), :] = x3 - 0.5 * (x2 + ahead)

    def quads(m):
        return [state[tile(m % SIDE, v), :] for v in range(QUADS)]

    put(0, quads(0))
    for node, index, stride in line_levels(CLEV):
        own, left, right = quads(node), quads(node - stride), quads(node + stride)
        put(index, [own[v] - 0.5 * (left[v] + right[v]) for v in range(QUADS)])


def column_dehier(natural, state):
    def get(index):
        base = index * SIDE
        x0 = sublane_dehier(natural[pl.ds(base, 8), :])
        ahead = pltpu.roll(x0, 7, 0)
        x2 = natural[pl.ds(base + 8, 8), :] + 0.5 * (x0 + ahead)
        x1 = natural[pl.ds(base + 16, 8, stride=2), :] + 0.5 * (x0 + x2)
        x3 = natural[pl.ds(base + 17, 8, stride=2), :] + 0.5 * (x2 + ahead)
        return [x0, x1, x2, x3]

    for v, x in enumerate(get(0)):
        state[tile(0, v), :] = x
    for node, index, stride in line_levels(CLEV):
        for v, x in enumerate(get(index)):
            left = state[tile((node - stride) % SIDE, v), :]
            right = state[tile((node + stride) % SIDE, v), :]
            state[tile(node, v), :] = x + 0.5 * (left + right)


CHUNK = 256


def first_kernel(devices, axis, start, cs, rs, levels, assign, forward, send, kept, speed, state, drift, csb):
    me = lax.axis_index(axis)
    level = levels[find_grid(assign, me)]
    total = start.shape[0]
    block_cols = total // devices
    fill_speed(cs, rs, level, csb, speed)
    fill_drift(speed, level, drift)
    for m in range(SIDE):
        for v in range(QUADS):
            state[0, tile(m, v), :] = start[spread(m, v), :]
    last = advance(state, drift, level, STEPS)
    matrix = forward[level - LMIN]
    for c in range(total // CHUNK):
        rows = pl.ds(c * CHUNK, CHUNK)
        kept[rows, :] = exact_dot(state[last, rows, :], matrix)
    for block in range(devices):
        for group, count in groups_of(block_cols):
            base = block * block_cols + group * 32
            tiles = [kept[pl.ds(base + 8 * k, 8), :] for k in range(count)]
            store_shared(send, block, block_cols, group, tiles)


def section_grids(levels, q):
    out = []
    for k in range(NLEV):
        found = jnp.int32(0)
        for j in range(NLEV):
            g = q * NLEV + j
            found = jnp.where(levels[g] == LMIN + k, g, found)
        out.append(found)
    return out


def section_weights(levels, coeffs, q):
    grids = section_grids(levels, q)
    w = [jnp.full((8, 128), coeffs[g].astype(jnp.float32)) for g in grids]
    lane = lanes()
    zero = jnp.zeros((8, 128), jnp.float32)

    def within(low, high, value):
        return jnp.where((lane >= low) & (lane < high), value, zero)

    two = [w[0], within(0, 64, w[1]), within(0, 32, w[2]), within(0, 16, w[3])]
    three = [w[1], within(64, 96, w[2]), within(64, 80, w[3])]
    four = [w[2], within(64, 96, w[3])]

    def scaled(parts):
        total = parts[0]
        for part in parts[1:]:
            total = total + part
        return [part / total for part in parts]

    return grids, scaled(two), scaled(three), scaled(four)


def combine_tile(s, two, three, four):
    x2 = (two[0] * s[0] + two[1] * s[1]) + (two[2] * s[2] + two[3] * s[3])
    d3 = three[0] * s[1] + (three[1] * pltpu.roll(s[2], 32, 1) + three[2] * pltpu.roll(s[3], 48, 1))
    d4 = four[0] * s[2] + four[1] * pltpu.roll(s[3], 32, 1)
    return x2, d3, d4


def level_tiles(x2, d3, d4, s5):
    lane = lanes()
    back3, back4 = pltpu.roll(d3, 96, 1), pltpu.roll(d4, 96, 1)
    low = lane < 64
    return [
        x2,
        jnp.where(low, x2, d3),
        jnp.where(lane < 32, x2, jnp.where(low, back3, d4)),
        jnp.where(
            lane < 16,
            x2,
            jnp.where(lane < 32, pltpu.roll(d3, 80, 1), jnp.where(low, back4, s5)),
        ),
    ]


def shared_kernel(block_cols, recv, levels, coeffs, assign, send):
    def section(q, carry):
        grids, two, three, four = section_weights(levels, coeffs, q)
        where = [assign[g] for g in grids]
        for group, count in groups_of(block_cols):
            parts = [load_shared(recv, d, block_cols, group, count) for d in where]
            made = []
            for t in range(count):
                s = [parts[k][t] for k in range(NLEV)]
                made.append(level_tiles(*combine_tile(s, two, three, four), s[3]))
            for k in range(NLEV):
                store_shared(send, where[k], block_cols, group, [made[t][k] for t in range(count)])
        return carry

    lax.fori_loop(0, recv.shape[0] // NLEV, section, jnp.int32(0))


def second_kernel(devices, axis, recv, kept, speed, levels, assign, owner, forward, backward, send, state, drift, natural):
    me = lax.axis_index(axis)
    level = levels[find_grid(assign, me)]
    total = kept.shape[0]
    block_cols = total // devices
    fill_drift(speed, level, drift)
    shared = lanes() < SHARED
    for block in range(devices):
        for group, count in groups_of(block_cols):
            tiles = load_shared(recv, block, block_cols, group, count)
            for t in range(count):
                rows = pl.ds(block * block_cols + group * 32 + 8 * t, 8)
                natural[rows, :] = jnp.where(shared, tiles[t], kept[rows, :])
    matrix = backward[level - LMIN]
    for c in range(total // CHUNK):
        rows = pl.ds(c * CHUNK, CHUNK)
        state[0, rows, :] = exact_dot(natural[rows, :], matrix)
    last = advance(state, drift, level, STEPS)
    column_hier(state.at[last], natural)
    matrix = forward[level - LMIN]
    size = max(block_cols, CHUNK)
    for c in range(total // size):
        values = exact_dot(natural[pl.ds(c * size, size), :], matrix)
        for k in range(size // block_cols):
            send[owner[c * (size // block_cols) + k], :, :] = values[k * block_cols : (k + 1) * block_cols]


def output_kernel(block_cols, recv, levels, coeffs, assign_from, assign_to, send, combined):
    low = lanes() < 64

    def pair(p, carry):
        both = [section_weights(levels, coeffs, 2 * p + k) for k in range(2)]
        for t in range(block_cols // 8):
            rows = pl.ds(t * 8, 8)
            made = []
            for grids, two, three, four in both:
                s = [recv[assign_from[g], rows, :] for g in grids]
                x2, d3, d4 = combine_tile(s, two, three, four)
                for g, one in zip(grids, level_tiles(x2, d3, d4, s[3])):
                    send[assign_to[g], rows, :] = one
                made.append((x2, d3, d4, s[3]))
            (xe, te, fe, se), (xo, to, fo, so) = made
            turned = pltpu.roll(xo, 64, 1)
            parts = [
                xe,
                jnp.where(low, pltpu.roll(te, 64, 1), fe),
                jnp.where(low, pltpu.roll(se, 64, 1), turned),
                jnp.where(low, turned, to),
                jnp.where(low, pltpu.roll(fo, 64, 1), so),
            ]
            for k, part in enumerate(parts):
                combined[rows, pl.ds(pl.multiple_of(p * 640 + k * 128, 128), 128)] = part
        return carry

    lax.fori_loop(0, recv.shape[0] // (2 * NLEV), pair, jnp.int32(0))


def last_kernel(devices, axis, recv, cs, rs, levels, assign, owner, backward, final, state, drift, natural, speed):
    me = lax.axis_index(axis)
    level = levels[find_grid(assign, me)]
    total = final.shape[0]
    block_cols = total // devices
    fill_speed(cs, rs, level, natural, speed)
    fill_drift(speed, level, drift)
    matrix = backward[level - LMIN]
    size = max(block_cols, CHUNK)
    for c in range(total // size):
        per = size // block_cols
        values = jnp.concatenate([recv[owner[c * per + k]] for k in range(per)], axis=0)
        natural[pl.ds(c * size, size), :] = exact_dot(values, matrix)
    column_dehier(natural, state.at[0])
    last = advance(state, drift, level, 1)
    for m in range(SIDE):
        for v in range(QUADS):
            final[spread(m, v), :] = state[last, tile(m, v), :]


def local(start_field, col_speed, row_speed, levels, coeffs, assign_first, assign_second, owner_of):
    forward, backward = row_tables()
    devices = lax.axis_size("grid")
    total, rows = start_field.shape[1:]
    block_cols = total // devices
    shared_rows = packed_rows(block_cols)
    sections = devices // NLEV
    section_rows = sum((2**LMIN if k == 0 else 2 ** (LMIN + k - 1)) * 2 ** (ROW_BITS - LMIN - k) for k in range(NLEV))
    cs = col_speed.reshape(-1, 128)

    def f32(*shape):
        return jax.ShapeDtypeStruct(shape, jnp.float32)

    field = (total, rows)
    state = pltpu.VMEM((2,) + field, jnp.float32)
    whole = pltpu.VMEM(field, jnp.float32)

    def exchange(blocks):
        return lax.all_to_all(blocks, "grid", split_axis=0, concat_axis=0, tiled=True)

    send, kept, speed = pl.pallas_call(
        functools.partial(first_kernel, devices, "grid"),
        name="first_cycle",
        out_shape=(f32(devices, shared_rows, rows), f32(*field), f32(*field)),
        in_specs=[VMEM, VMEM, SMEM, SMEM, SMEM, VMEM],
        out_specs=(VMEM, VMEM, VMEM),
        scratch_shapes=[state, state, whole],
    )(start_field[0], cs, row_speed, levels, assign_first, forward)
    recv = exchange(send)
    send = pl.pallas_call(
        functools.partial(shared_kernel, block_cols),
        name="shared_rows",
        out_shape=f32(devices, shared_rows, rows),
        in_specs=[VMEM, SMEM, SMEM, SMEM],
        out_specs=VMEM,
    )(recv, levels, coeffs, assign_first)
    recv = exchange(send)
    send = pl.pallas_call(
        functools.partial(second_kernel, devices, "grid"),
        name="second_cycle",
        out_shape=f32(devices, block_cols, rows),
        in_specs=[VMEM, VMEM, VMEM, SMEM, SMEM, SMEM, VMEM, VMEM],
        out_specs=VMEM,
        scratch_shapes=[state, state, whole],
    )(recv, kept, speed, levels, assign_first, owner_of, forward, backward)
    recv = exchange(send)
    send, combined = pl.pallas_call(
        functools.partial(output_kernel, block_cols),
        name="second_combined",
        out_shape=(f32(devices, block_cols, rows), f32(block_cols, sections * section_rows)),
        in_specs=[VMEM, SMEM, SMEM, SMEM, SMEM],
        out_specs=(VMEM, VMEM),
    )(recv, levels, coeffs, assign_first, assign_second)
    recv = exchange(send)
    final = pl.pallas_call(
        functools.partial(last_kernel, devices, "grid"),
        name="last_step",
        out_shape=f32(*field),
        in_specs=[VMEM, VMEM, SMEM, SMEM, SMEM, SMEM, VMEM],
        out_specs=VMEM,
        scratch_shapes=[state, state, whole, whole],
    )(recv, cs, row_speed, levels, assign_second, owner_of, backward)
    return combined, final[None]


def solution(mesh):
    placed = (
        P(("groups", "grid"), None, None),
        P(),
        P(),
        P("groups"),
        P("groups"),
        P("groups"),
        P("groups"),
        P("groups"),
    )
    return jax.shard_map(
        local,
        mesh=mesh,
        in_specs=placed,
        out_specs=(P(("groups", "grid"), None), P(("groups", "grid"), None, None)),
        check_vma=False,
    )
```

time: 270 us -> 121 us (0.45)
  the two profiles are of different devices: /device:TPU:20 before, /device:TPU:16 now
where the time goes in v1:
time: 121 us
  blocking collectives  84.4 us (70%)
  Pallas kernels  35.7 us (30%)
    all_to_all x4, blocking collectives, exchange(): lax.all_to_all(blocks, 'grid', split_axis=0, concat_axis=0, tiled=True)  84.4 us
    pallas_call x1, Pallas kernels, local(): pl.pallas_call(functools.partial(second_kernel, devices, 'grid'), name='s...  10.4 us
    pallas_call x1, Pallas kernels, local(): pl.pallas_call(functools.partial(first_kernel, devices, 'grid'), name='fi...  10 us
    pallas_call x1, Pallas kernels, local(): pl.pallas_call(functools.partial(last_kernel, devices, 'grid'), name='las...  9.64 us
    pallas_call x1, Pallas kernels, local(): pl.pallas_call(functools.partial(shared_kernel, block_cols), name='shared...  3.08 us
    pallas_call x1, Pallas kernels, local(): pl.pallas_call(functools.partial(output_kernel, block_cols), name='second...  2.52 us

profile of v1, /device:TPU:16, one launch (start us, length us, event | category | flops | bytes accessed | tf_op | source)
XLA Modules:
  0.0 120.7 jit_solution(7516289107842686092)
XLA Ops:
  0.6 10.0 %first_cycle.1 = (f32[16,48,128]{2,1,0:T(8,128)}, f32[1024,128]{1,0:T(8,128)}, f32[1024,128]{1,0:T(8,128)}) custom-call(f32[1024,128]{1,0:T(8,128)} %bitcast.3, f32[8,128]{1,0:T(8,128)} %bitcast.5, f32[32]{0:T(128)} %rs.3, s32[16]{0:T(128)} %levels.9, s32[16]{0:T(128)} %assign_from.1, bf16[4,128,128]{2,1,0:T(8,128)(2,1)} %constant.4.clone.forward), custom_call_target="tpu_custom_call" | custom-call | tf_op jit(solution)/shard_map/first_cycle/pallas_call | solution.py:499
  10.7 23.3 %all_to_all.20.recv = f32[16,48,128]{2,1,0:T(8,128)} all-to-all(f32[16,48,128]{2,1,0:T(8,128)} %get-tuple-element.7), channel_id=1, replica_groups=mesh['groups'=2,'grid'=16] {'grid'}, dimensions={0} | all-to-all | bytes 786432 | tf_op jit(solution)/shard_map/all_to_all | solution.py:497
  34.0 3.1 %shared_rows.1 = f32[16,48,128]{2,1,0:T(8,128)} custom-call(f32[16,48,128]{2,1,0:T(8,128)} %all_to_all.20.recv, s32[16]{0:T(128)} %levels.9, s32[16]{0:T(128)} %coeffs.3, s32[16]{0:T(128)} %assign_from.1), custom_call_target="tpu_custom_call" | custom-call | tf_op jit(solution)/shard_map/shared_rows/pallas_call | solution.py:508
  37.1 16.3 %all_to_all.21.recv = f32[16,48,128]{2,1,0:T(8,128)} all-to-all(f32[16,48,128]{2,1,0:T(8,128)} %shared_rows.1), channel_id=1, replica_groups=mesh['groups'=2,'grid'=16] {'grid'}, dimensions={0} | all-to-all | bytes 786432 | tf_op jit(solution)/shard_map/all_to_all | solution.py:497
  53.4 10.4 %second_cycle.1 = f32[16,64,128]{2,1,0:T(8,128)} custom-call(f32[16,48,128]{2,1,0:T(8,128)} %all_to_all.21.recv, f32[1024,128]{1,0:T(8,128)} %get-tuple-element.8.kept, f32[1024,128]{1,0:T(8,128)} %get-tuple-element.9.speed, s32[16]{0:T(128)} %levels.9, s32[16]{0:T(128)} %assign_from.1, s32[16]{0:T(128)} %owner.3, ...), custom_call_target="tpu_custom_call" | custom-call | tf_op jit(solution)/shard_map/second_cycle/pallas_call | solution.py:516
  63.8 26.3 %all_to_all.22.recv = f32[16,64,128]{2,1,0:T(8,128)} all-to-all(f32[16,64,128]{2,1,0:T(8,128)} %second_cycle.1), channel_id=1, replica_groups=mesh['groups'=2,'grid'=16] {'grid'}, dimensions={0} | all-to-all | bytes 1048576 | tf_op jit(solution)/shard_map/all_to_all | solution.py:497
  90.1 2.5 %second_combined.1 = (f32[16,64,128]{2,1,0:T(8,128)}, f32[64,1280]{1,0:T(8,128)}) custom-call(f32[16,64,128]{2,1,0:T(8,128)} %all_to_all.22.recv, s32[16]{0:T(128)} %levels.9, s32[16]{0:T(128)} %coeffs.3, s32[16]{0:T(128)} %assign_from.1, s32[16]{0:T(128)} %assign.7), custom_call_target="tpu_custom_call" | custom-call | tf_op jit(solution)/shard_map/second_combined/pallas_call | solution.py:525
  92.6 18.5 %all_to_all.23.recv = f32[16,64,128]{2,1,0:T(8,128)} all-to-all(f32[16,64,128]{2,1,0:T(8,128)} %get-tuple-element.11), channel_id=1, replica_groups=mesh['groups'=2,'grid'=16] {'grid'}, dimensions={0} | all-to-all | bytes 1048576 | tf_op jit(solution)/shard_map/all_to_all | solution.py:497
  111.1 9.6 %last_step.1 = f32[1024,128]{1,0:T(8,128)} custom-call(f32[16,64,128]{2,1,0:T(8,128)} %all_to_all.23.recv, f32[8,128]{1,0:T(8,128)} %bitcast.6, f32[32]{0:T(128)} %rs.3, s32[16]{0:T(128)} %levels.9, s32[16]{0:T(128)} %assign.7, s32[16]{0:T(128)} %owner.3, bf16[4,128,128]{2,1,0:T(8,128)(2,1)} %constant.5.clone.backward), custom_call_target="tpu_custom_call" | custom-call | tf_op jit(solution)/shard_map/last_step/pallas_call | solution.py:533

commit v2 on v1

--- a/solution.py
+++ b/solution.py
@@ -20,6 +20,7 @@
 QUADS = SIDE // 8
 ROW_BITS = 2 * LMIN + NLEV - 1
 SHARED = 96
+PLANES = 8
 SMEM = pl.BlockSpec(memory_space=pltpu.SMEM)
 VMEM = pl.BlockSpec(memory_space=pltpu.VMEM)
 
@@ -75,6 +76,19 @@
     )
 
 
+def row_stencils():
+    out = []
+    for k in range(NLEV):
+        first, second = LMIN + k, ROW_BITS - LMIN - k
+        eye_one, eye_two = np.eye(2**first), np.eye(2**second)
+        up_one, down_one = (np.kron(np.roll(eye_one, s, 0), eye_two) for s in (1, -1))
+        up_two, down_two = (np.kron(eye_one, np.roll(eye_two, s, 0)) for s in (1, -1))
+        near = 4.0 ** (first - CLEV) * (up_one + down_one) + 4.0 ** (second - CLEV) * (up_two + down_two)
+        both = np.concatenate([near, up_one - down_one], axis=1)
+        out.append(np.concatenate([both, both], axis=0))
+    return jnp.asarray(np.stack(out), jnp.bfloat16)
+
+
 def pick(level, values):
     out = jnp.float32(values[0])
     for k in range(1, NLEV):
@@ -119,61 +133,54 @@
             speed[tile(m, v), :] = csb[spread(m, v), :] * factor
 
 
-def fill_drift(speed, level, drift):
-    along = pick(level, [diffusivity * time_step * 4 ** (LMIN + k) / 2**k for k in range(NLEV)])
-    for t in range(SIDE * QUADS):
-        rows = pl.ds(t * 8, 8)
-        one = speed[rows, :]
-        drift[0, rows, :] = along - one
-        drift[1, rows, :] = along + one
-
-
-def advance(state, drift, level, count):
-    other = ROW_BITS - level
-    inner = jnp.left_shift(jnp.int32(1), other)
+def split(values):
+    high = values.astype(jnp.bfloat16)
+    middle = (values - high.astype(jnp.float32)).astype(jnp.bfloat16)
+    return jnp.concatenate([high, middle], axis=1)
+
+
+def one_substep(source, target, speed, weights, coef_col, coef_own):
+    def plane(m):
+        return source[pl.ds((m % SIDE) * SIDE, SIDE), :]
+
+    below, mid = plane(SIDE - 1), plane(0)
+    for first in range(0, SIDE, PLANES):
+        pieces = split(source[pl.ds(first * SIDE, PLANES * SIDE), :])
+        along = jnp.dot(pieces, weights, preferred_element_type=jnp.float32)
+        for m in range(first, first + PLANES):
+            above = plane(m + 1)
+            part = along[(m - first) * SIDE : (m - first + 1) * SIDE]
+            ahead = jnp.concatenate([mid[8:], pltpu.roll(mid[:8], 7, 0)], axis=0)
+            behind = jnp.concatenate([pltpu.roll(mid[SIDE - 8 :], 1, 0), mid[: SIDE - 8]], axis=0)
+            around = (above + below) + (ahead + behind) + part[:, :128]
+            rows = pl.ds(m * SIDE, SIDE)
+            target[rows, :] = coef_own * mid + coef_col * around - speed[rows, :] * part[:, 128:]
+            below, mid = mid, above
+
+
+def advance(state, spare, speed, stencil, level, count):
     refine = jnp.left_shift(jnp.int32(1), level - LMIN)
     across = [diffusivity * time_step * 4 ** (ROW_BITS - LMIN - k) / 2**k for k in range(NLEV)]
     along = [diffusivity * time_step * 4 ** (LMIN + k) / 2**k for k in range(NLEV)]
     outer = [diffusivity * time_step * 4**CLEV / 2**k for k in range(NLEV)]
     keep = [1.0 - 2.0 * across[k] - 2.0 * along[k] - 4.0 * outer[k] for k in range(NLEV)]
-    coef_two = pick(level, across)
     coef_col = pick(level, outer)
     coef_own = pick(level, keep)
-    shape = (SIDE, 128)
-    lane = lax.broadcasted_iota(jnp.int32, shape, 1)
-    place = jnp.bitwise_and(lane, inner - 1)
-    at_last = place == inner - 1
-    at_first = place == 0
-
-    def one_substep(step, carry):
-        now = jnp.bitwise_and(step, 1)
-        later = 1 - now
-        src = state.at[now]
-        dst = state.at[later]
-
-        def plane(m):
-            return src[pl.ds((m % SIDE) * SIDE, SIDE), :]
-
-        below, mid = plane(SIDE - 1), plane(0)
-        for m in range(SIDE):
-            above = plane(m + 1)
-            rows = pl.ds(m * SIDE, SIDE)
-            acc = coef_own * mid
-            acc += drift[0, rows, :] * pltpu.roll(mid, 128 - inner, 1)
-            acc += drift[1, rows, :] * pltpu.roll(mid, inner, 1)
-            up = jnp.where(at_last, pltpu.roll(mid, inner - 1, 1), pltpu.roll(mid, 127, 1))
-            down = jnp.where(at_first, pltpu.roll(mid, 129 - inner, 1), pltpu.roll(mid, 1, 1))
-            acc += coef_two * (up + down)
-            ahead = jnp.concatenate([mid[8:], pltpu.roll(mid[:8], 7, 0)], axis=0)
-            behind = jnp.concatenate([pltpu.roll(mid[SIDE - 8 :], 1, 0), mid[: SIDE - 8]], axis=0)
-            acc += coef_col * ((above + below) + (ahead + behind))
-            dst[rows, :] = acc
-            below, mid = mid, above
+    weights = stencil[level - LMIN]
+    steps = refine * count
+
+    def two(step, carry):
+        one_substep(state, spare, speed, weights, coef_col, coef_own)
+        one_substep(spare, state, speed, weights, coef_col, coef_own)
         return carry
 
-    steps = refine * count
-    lax.fori_loop(0, steps, one_substep, jnp.int32(0))
-    return jnp.bitwise_and(steps, 1)
+    lax.fori_loop(0, jnp.right_shift(steps, 1), two, jnp.int32(0))
+    if count % 2:
+
+        @pl.when(jnp.bitwise_and(steps, 1) == 1)
+        def _():
+            one_substep(state, spare, speed, weights, coef_col, coef_own)
+            state[...] = spare[...]
 
 
 def exact_dot(values, matrix):
@@ -304,21 +311,20 @@
 CHUNK = 256
 
 
-def first_kernel(devices, axis, start, cs, rs, levels, assign, forward, send, kept, speed, state, drift, csb):
+def first_kernel(devices, axis, start, cs, rs, levels, assign, forward, stencil, send, kept, speed, state, spare):
     me = lax.axis_index(axis)
     level = levels[find_grid(assign, me)]
     total = start.shape[0]
     block_cols = total // devices
-    fill_speed(cs, rs, level, csb, speed)
-    fill_drift(speed, level, drift)
+    fill_speed(cs, rs, level, spare, speed)
     for m in range(SIDE):
         for v in range(QUADS):
-            state[0, tile(m, v), :] = start[spread(m, v), :]
-    last = advance(state, drift, level, STEPS)
+            state[tile(m, v), :] = start[spread(m, v), :]
+    advance(state, spare, speed, stencil, level, STEPS)
     matrix = forward[level - LMIN]
     for c in range(total // CHUNK):
         rows = pl.ds(c * CHUNK, CHUNK)
-        kept[rows, :] = exact_dot(state[last, rows, :], matrix)
+        kept[rows, :] = exact_dot(state[rows, :], matrix)
     for block in range(devices):
         for group, count in groups_of(block_cols):
             base = block * block_cols + group * 32
@@ -399,12 +405,11 @@
     lax.fori_loop(0, recv.shape[0] // NLEV, section, jnp.int32(0))
 
 
-def second_kernel(devices, axis, recv, kept, speed, levels, assign, owner, forward, backward, send, state, drift, natural):
+def second_kernel(devices, axis, recv, kept, speed, levels, assign, owner, forward, backward, stencil, send, state, spare, natural):
     me = lax.axis_index(axis)
     level = levels[find_grid(assign, me)]
     total = kept.shape[0]
     block_cols = total // devices
-    fill_drift(speed, level, drift)
     shared = lanes() < SHARED
     for block in range(devices):
         for group, count in groups_of(block_cols):
@@ -415,9 +420,9 @@
     matrix = backward[level - LMIN]
     for c in range(total // CHUNK):
         rows = pl.ds(c * CHUNK, CHUNK)
-        state[0, rows, :] = exact_dot(natural[rows, :], matrix)
-    last = advance(state, drift, level, STEPS)
-    column_hier(state.at[last], natural)
+        state[rows, :] = exact_dot(natural[rows, :], matrix)
+    advance(state, spare, speed, stencil, level, STEPS)
+    column_hier(state, natural)
     matrix = forward[level - LMIN]
     size = max(block_cols, CHUNK)
     for c in range(total // size):
@@ -456,28 +461,28 @@
     lax.fori_loop(0, recv.shape[0] // (2 * NLEV), pair, jnp.int32(0))
 
 
-def last_kernel(devices, axis, recv, cs, rs, levels, assign, owner, backward, final, state, drift, natural, speed):
+def last_kernel(devices, axis, recv, cs, rs, levels, assign, owner, backward, stencil, final, state, spare, natural, speed):
     me = lax.axis_index(axis)
     level = levels[find_grid(assign, me)]
     total = final.shape[0]
     block_cols = total // devices
     fill_speed(cs, rs, level, natural, speed)
-    fill_drift(speed, level, drift)
     matrix = backward[level - LMIN]
     size = max(block_cols, CHUNK)
     for c in range(total // size):
         per = size // block_cols
         values = jnp.concatenate([recv[owner[c * per + k]] for k in range(per)], axis=0)
         natural[pl.ds(c * size, size), :] = exact_dot(values, matrix)
-    column_dehier(natural, state.at[0])
-    last = advance(state, drift, level, 1)
+    column_dehier(natural, state)
+    advance(state, spare, speed, stencil, level, 1)
     for m in range(SIDE):
         for v in range(QUADS):
-            final[spread(m, v), :] = state[last, tile(m, v), :]
+            final[spread(m, v), :] = state[tile(m, v), :]
 
 
 def local(start_field, col_speed, row_speed, levels, coeffs, assign_first, assign_second, owner_of):
     forward, backward = row_tables()
+    stencil = row_stencils()
     devices = lax.axis_size("grid")
     total, rows = start_field.shape[1:]
     block_cols = total // devices
@@ -490,7 +495,6 @@
         return jax.ShapeDtypeStruct(shape, jnp.float32)
 
     field = (total, rows)
-    state = pltpu.VMEM((2,) + field, jnp.float32)
     whole = pltpu.VMEM(field, jnp.float32)
 
     def exchange(blocks):
@@ -500,10 +504,10 @@
         functools.partial(first_kernel, devices, "grid"),
         name="first_cycle",
         out_shape=(f32(devices, shared_rows, rows), f32(*field), f32(*field)),
-        in_specs=[VMEM, VMEM, SMEM, SMEM, SMEM, VMEM],
+        in_specs=[VMEM, VMEM, SMEM, SMEM, SMEM, VMEM, VMEM],
         out_specs=(VMEM, VMEM, VMEM),
-        scratch_shapes=[state, state, whole],
-    )(start_field[0], cs, row_speed, levels, assign_first, forward)
+        scratch_shapes=[whole, whole],
+    )(start_field[0], cs, row_speed, levels, assign_first, forward, stencil)
     recv = exchange(send)
     send = pl.pallas_call(
         functools.partial(shared_kernel, block_cols),
@@ -517,10 +521,10 @@
         functools.partial(second_kernel, devices, "grid"),
         name="second_cycle",
         out_shape=f32(devices, block_cols, rows),
-        in_specs=[VMEM, VMEM, VMEM, SMEM, SMEM, SMEM, VMEM, VMEM],
+        in_specs=[VMEM, VMEM, VMEM, SMEM, SMEM, SMEM, VMEM, VMEM, VMEM],
         out_specs=VMEM,
-        scratch_shapes=[state, state, whole],
-    )(recv, kept, speed, levels, assign_first, owner_of, forward, backward)
+        scratch_shapes=[whole, whole, whole],
+    )(recv, kept, speed, levels, assign_first, owner_of, forward, backward, stencil)
     recv = exchange(send)
     send, combined = pl.pallas_call(
         functools.partial(output_kernel, block_cols),
@@ -534,10 +538,10 @@
         functools.partial(last_kernel, devices, "grid"),
         name="last_step",
         out_shape=f32(*field),
-        in_specs=[VMEM, VMEM, SMEM, SMEM, SMEM, SMEM, VMEM],
+        in_specs=[VMEM, VMEM, SMEM, SMEM, SMEM, SMEM, VMEM, VMEM],
         out_specs=VMEM,
-        scratch_shapes=[state, state, whole, whole],
-    )(recv, cs, row_speed, levels, assign_second, owner_of, backward)
+        scratch_shapes=[whole, whole, whole, whole],
+    )(recv, cs, row_speed, levels, assign_second, owner_of, backward, stencil)
     return combined, final[None]
 
 

time: 121 us -> 99.4 us (0.82)
  the two profiles are of different devices: /device:TPU:16 before, /device:TPU:1 now
where the time goes in v2:
time: 99.4 us; the launch traced here: 98.8 us
  blocking collectives  78.7 us (79%)
  Pallas kernels  19.5 us (20%)
    all_to_all x4, blocking collectives, exchange(): lax.all_to_all(blocks, 'grid', split_axis=0, concat_axis=0, tiled=True)  78.7 us
    pallas_call x1, Pallas kernels, local(): pl.pallas_call(functools.partial(last_kernel, devices, 'grid'), name='las...  4.99 us
    pallas_call x1, Pallas kernels, local(): pl.pallas_call(functools.partial(second_kernel, devices, 'grid'), name='s...  4.6 us
    pallas_call x1, Pallas kernels, local(): pl.pallas_call(functools.partial(first_kernel, devices, 'grid'), name='fi...  4.28 us
    pallas_call x1, Pallas kernels, local(): pl.pallas_call(functools.partial(shared_kernel, block_cols), name='shared...  3.08 us
    pallas_call x1, Pallas kernels, local(): pl.pallas_call(functools.partial(output_kernel, block_cols), name='second...  2.52 us

profile of v2, /device:TPU:1, one launch (start us, length us, event | category | flops | bytes accessed | tf_op | source)
XLA Modules:
  0.0 98.8 jit_solution(12034954130993193594)
XLA Ops:
  0.6 4.3 %first_cycle.1 = (f32[16,48,128]{2,1,0:T(8,128)}, f32[1024,128]{1,0:T(8,128)}, f32[1024,128]{1,0:T(8,128)}) custom-call(f32[1024,128]{1,0:T(8,128)} %bitcast.3, f32[8,128]{1,0:T(8,128)} %bitcast.5, f32[32]{0:T(128)} %rs.3, s32[16]{0:T(128)} %levels.9, s32[16]{0:T(128)} %assign_from.1, bf16[4,128,128]{2,1,0:T(8,128)(2,1)} %constant.6.clone.forward, ...), custom_call_target="tpu_custom_call" | custom-call | tf_op jit(solution)/shard_map/first_cycle/pallas_call | solution.py:503
  4.9 22.7 %all_to_all.20.recv = f32[16,48,128]{2,1,0:T(8,128)} all-to-all(f32[16,48,128]{2,1,0:T(8,128)} %get-tuple-element.7), channel_id=1, replica_groups=mesh['groups'=2,'grid'=16] {'grid'}, dimensions={0} | all-to-all | bytes 786432 | tf_op jit(solution)/shard_map/all_to_all | solution.py:501
  27.6 3.1 %shared_rows.1 = f32[16,48,128]{2,1,0:T(8,128)} custom-call(f32[16,48,128]{2,1,0:T(8,128)} %all_to_all.20.recv, s32[16]{0:T(128)} %levels.9, s32[16]{0:T(128)} %coeffs.3, s32[16]{0:T(128)} %assign_from.1), custom_call_target="tpu_custom_call" | custom-call | tf_op jit(solution)/shard_map/shared_rows/pallas_call | solution.py:512
  30.7 16.4 %all_to_all.21.recv = f32[16,48,128]{2,1,0:T(8,128)} all-to-all(f32[16,48,128]{2,1,0:T(8,128)} %shared_rows.1), channel_id=1, replica_groups=mesh['groups'=2,'grid'=16] {'grid'}, dimensions={0} | all-to-all | bytes 786432 | tf_op jit(solution)/shard_map/all_to_all | solution.py:501
  47.1 4.6 %second_cycle.1 = f32[16,64,128]{2,1,0:T(8,128)} custom-call(f32[16,48,128]{2,1,0:T(8,128)} %all_to_all.21.recv, f32[1024,128]{1,0:T(8,128)} %get-tuple-element.8.kept, f32[1024,128]{1,0:T(8,128)} %get-tuple-element.9.speed, s32[16]{0:T(128)} %levels.9, s32[16]{0:T(128)} %assign_from.1, s32[16]{0:T(128)} %owner.3, ...), custom_call_target="tpu_custom_call" | custom-call | tf_op jit(solution)/shard_map/second_cycle/pallas_call | solution.py:520
  51.7 21.1 %all_to_all.22.recv = f32[16,64,128]{2,1,0:T(8,128)} all-to-all(f32[16,64,128]{2,1,0:T(8,128)} %second_cycle.1), channel_id=1, replica_groups=mesh['groups'=2,'grid'=16] {'grid'}, dimensions={0} | all-to-all | bytes 1048576 | tf_op jit(solution)/shard_map/all_to_all | solution.py:501
  72.8 2.5 %second_combined.1 = (f32[16,64,128]{2,1,0:T(8,128)}, f32[64,1280]{1,0:T(8,128)}) custom-call(f32[16,64,128]{2,1,0:T(8,128)} %all_to_all.22.recv, s32[16]{0:T(128)} %levels.9, s32[16]{0:T(128)} %coeffs.3, s32[16]{0:T(128)} %assign_from.1, s32[16]{0:T(128)} %assign.7), custom_call_target="tpu_custom_call" | custom-call | tf_op jit(solution)/shard_map/second_combined/pallas_call | solution.py:529
  75.3 18.5 %all_to_all.23.recv = f32[16,64,128]{2,1,0:T(8,128)} all-to-all(f32[16,64,128]{2,1,0:T(8,128)} %get-tuple-element.11), channel_id=1, replica_groups=mesh['groups'=2,'grid'=16] {'grid'}, dimensions={0} | all-to-all | bytes 1048576 | tf_op jit(solution)/shard_map/all_to_all | solution.py:501
  93.8 5.0 %last_step.1 = f32[1024,128]{1,0:T(8,128)} custom-call(f32[16,64,128]{2,1,0:T(8,128)} %all_to_all.23.recv, f32[8,128]{1,0:T(8,128)} %bitcast.6, f32[32]{0:T(128)} %rs.3, s32[16]{0:T(128)} %levels.9, s32[16]{0:T(128)} %assign.7, s32[16]{0:T(128)} %owner.3, bf16[4,128,128]{2,1,0:T(8,128)(2,1)} %constant.7.clone.backward, ...), custom_call_target="tpu_custom_call" | custom-call | tf_op jit(solution)/shard_map/last_step/pallas_call | solution.py:537

commit v3 on v2

--- a/solution.py
+++ b/solution.py
@@ -21,8 +21,10 @@
 ROW_BITS = 2 * LMIN + NLEV - 1
 SHARED = 96
 PLANES = 8
+PARAMS = pltpu.CompilerParams(vmem_limit_bytes=12 * 2**20)
 SMEM = pl.BlockSpec(memory_space=pltpu.SMEM)
 VMEM = pl.BlockSpec(memory_space=pltpu.VMEM)
+HBM = pl.BlockSpec(memory_space=pltpu.HBM)
 
 
 def hier_line(line_level):
@@ -166,7 +168,7 @@
     keep = [1.0 - 2.0 * across[k] - 2.0 * along[k] - 4.0 * outer[k] for k in range(NLEV)]
     coef_col = pick(level, outer)
     coef_own = pick(level, keep)
-    weights = stencil[level - LMIN]
+    weights = stencil[...]
     steps = refine * count
 
     def two(step, carry):
@@ -181,6 +183,10 @@
         def _():
             one_substep(state, spare, speed, weights, coef_col, coef_own)
             state[...] = spare[...]
+
+
+def in_hbm(x):
+    return pltpu.with_memory_space_constraint(x, pltpu.HBM)
 
 
 def exact_dot(values, matrix):
@@ -311,17 +317,59 @@
 CHUNK = 256
 
 
-def first_kernel(devices, axis, start, cs, rs, levels, assign, forward, stencil, send, kept, speed, state, spare):
+def first_kernel(
+    devices,
+    axis,
+    start_hbm,
+    cs_hbm,
+    rs_hbm,
+    levels_hbm,
+    assign_hbm,
+    forward_hbm,
+    stencil_hbm,
+    send,
+    kept,
+    speed,
+    state,
+    spare,
+    start,
+    cs,
+    forward,
+    stencil,
+    rs,
+    levels,
+    assign,
+    sems,
+):
+    def copy(k, source, target):
+        one = pltpu.make_async_copy(source, target, sems.at[k])
+        one.start()
+        return one
+
+    ints = [copy(0, levels_hbm, levels), copy(1, assign_hbm, assign)]
+    speeds = [copy(2, rs_hbm, rs), copy(3, cs_hbm, cs)]
+    values = copy(4, start_hbm, start)
+    for one in ints:
+        one.wait()
     me = lax.axis_index(axis)
     level = levels[find_grid(assign, me)]
+    tables = [
+        copy(5, stencil_hbm.at[level - LMIN], stencil),
+        copy(6, forward_hbm.at[level - LMIN], forward),
+    ]
     total = start.shape[0]
     block_cols = total // devices
+    for one in speeds:
+        one.wait()
     fill_speed(cs, rs, level, spare, speed)
+    values.wait()
     for m in range(SIDE):
         for v in range(QUADS):
             state[tile(m, v), :] = start[spread(m, v), :]
+    for one in tables:
+        one.wait()
     advance(state, spare, speed, stencil, level, STEPS)
-    matrix = forward[level - LMIN]
+    matrix = forward[...]
     for c in range(total // CHUNK):
         rows = pl.ds(c * CHUNK, CHUNK)
         kept[rows, :] = exact_dot(state[rows, :], matrix)
@@ -405,7 +453,9 @@
     lax.fori_loop(0, recv.shape[0] // NLEV, section, jnp.int32(0))
 
 
-def second_kernel(devices, axis, recv, kept, speed, levels, assign, owner, forward, backward, stencil, send, state, spare, natural):
+def second_kernel(devices, axis, recv, kept, speed, levels, assign, owner_hbm, forward, backward, stencil, send, state, spare, natural, owner, sem):
+    owners = pltpu.make_async_copy(owner_hbm, owner, sem)
+    owners.start()
     me = lax.axis_index(axis)
     level = levels[find_grid(assign, me)]
     total = kept.shape[0]
@@ -421,8 +471,9 @@
     for c in range(total // CHUNK):
         rows = pl.ds(c * CHUNK, CHUNK)
         state[rows, :] = exact_dot(natural[rows, :], matrix)
-    advance(state, spare, speed, stencil, level, STEPS)
+    advance(state, spare, speed, stencil.at[level - LMIN], level, STEPS)
     column_hier(state, natural)
+    owners.wait()
     matrix = forward[level - LMIN]
     size = max(block_cols, CHUNK)
     for c in range(total // size):
@@ -474,7 +525,7 @@
         values = jnp.concatenate([recv[owner[c * per + k]] for k in range(per)], axis=0)
         natural[pl.ds(c * size, size), :] = exact_dot(values, matrix)
     column_dehier(natural, state)
-    advance(state, spare, speed, stencil, level, 1)
+    advance(state, spare, speed, stencil.at[level - LMIN], level, 1)
     for m in range(SIDE):
         for v in range(QUADS):
             final[spread(m, v), :] = state[tile(m, v), :]
@@ -500,18 +551,32 @@
     def exchange(blocks):
         return lax.all_to_all(blocks, "grid", split_axis=0, concat_axis=0, tiled=True)
 
+    first_args = (start_field[0], cs, row_speed, levels, assign_first, forward, stencil)
     send, kept, speed = pl.pallas_call(
         functools.partial(first_kernel, devices, "grid"),
         name="first_cycle",
+        compiler_params=PARAMS,
         out_shape=(f32(devices, shared_rows, rows), f32(*field), f32(*field)),
-        in_specs=[VMEM, VMEM, SMEM, SMEM, SMEM, VMEM, VMEM],
+        in_specs=[HBM] * 7,
         out_specs=(VMEM, VMEM, VMEM),
-        scratch_shapes=[whole, whole],
-    )(start_field[0], cs, row_speed, levels, assign_first, forward, stencil)
+        scratch_shapes=[
+            whole,
+            whole,
+            whole,
+            pltpu.VMEM(cs.shape, jnp.float32),
+            pltpu.VMEM(forward.shape[1:], jnp.bfloat16),
+            pltpu.VMEM(stencil.shape[1:], jnp.bfloat16),
+            pltpu.SMEM(row_speed.shape, jnp.float32),
+            pltpu.SMEM(levels.shape, jnp.int32),
+            pltpu.SMEM(levels.shape, jnp.int32),
+            pltpu.SemaphoreType.DMA((7,)),
+        ],
+    )(*(in_hbm(x) for x in first_args))
     recv = exchange(send)
     send = pl.pallas_call(
         functools.partial(shared_kernel, block_cols),
         name="shared_rows",
+        compiler_params=PARAMS,
         out_shape=f32(devices, shared_rows, rows),
         in_specs=[VMEM, SMEM, SMEM, SMEM],
         out_specs=VMEM,
@@ -520,15 +585,17 @@
     send = pl.pallas_call(
         functools.partial(second_kernel, devices, "grid"),
         name="second_cycle",
+        compiler_params=PARAMS,
         out_shape=f32(devices, block_cols, rows),
-        in_specs=[VMEM, VMEM, VMEM, SMEM, SMEM, SMEM, VMEM, VMEM, VMEM],
+        in_specs=[VMEM, VMEM, VMEM, SMEM, SMEM, HBM, VMEM, VMEM, VMEM],
         out_specs=VMEM,
-        scratch_shapes=[whole, whole, whole],
-    )(recv, kept, speed, levels, assign_first, owner_of, forward, backward, stencil)
+        scratch_shapes=[whole, whole, whole, pltpu.SMEM(owner_of.shape, jnp.int32), pltpu.SemaphoreType.DMA],
+    )(recv, kept, speed, levels, assign_first, in_hbm(owner_of), forward, backward, stencil)
     recv = exchange(send)
     send, combined = pl.pallas_call(
         functools.partial(output_kernel, block_cols),
         name="second_combined",
+        compiler_params=PARAMS,
         out_shape=(f32(devices, block_cols, rows), f32(block_cols, sections * section_rows)),
         in_specs=[VMEM, SMEM, SMEM, SMEM, SMEM],
         out_specs=(VMEM, VMEM),
@@ -537,6 +604,7 @@
     final = pl.pallas_call(
         functools.partial(last_kernel, devices, "grid"),
         name="last_step",
+        compiler_params=PARAMS,
         out_shape=f32(*field),
         in_specs=[VMEM, VMEM, SMEM, SMEM, SMEM, SMEM, VMEM, VMEM],
         out_specs=VMEM,

time: 99.4 us -> 92.3 us (0.929)
  blocking collectives: 78.7 us -> 70.5 us
  Pallas kernels: 19.5 us -> 20.6 us
    all_to_all x4, blocking collectives: 78.7 us -> 70.5 us  [exchange(): lax.all_to_all(blocks, 'grid', split_axis=0, concat_axis=0, tiled=True)]
    pallas_call x1, Pallas kernels: 4.28 us -> 7.13 us  [local(): pl.pallas_call(functools.partial(first_kernel, devices, 'grid'), name='fi...]
    pallas_call x1, Pallas kernels: 4.6 us -> 6.55 us  [local(): pl.pallas_call(functools.partial(second_kernel, devices, 'grid'), name='s...]
    pallas_call x1, Pallas kernels: 4.99 us -> 3.16 us  [local(): pl.pallas_call(functools.partial(last_kernel, devices, 'grid'), name='las...]
    pallas_call x1, Pallas kernels: 3.08 us -> 1.88 us  [local(): pl.pallas_call(functools.partial(shared_kernel, block_cols), name='shared...]
where the time goes in v3:
time: 92.3 us; the launch traced here: 91.8 us
  blocking collectives  70.5 us (76%)
  Pallas kernels  20.6 us (22%)
    all_to_all x4, blocking collectives, exchange(): lax.all_to_all(blocks, 'grid', split_axis=0, concat_axis=0, tiled=True)  70.5 us
    pallas_call x1, Pallas kernels, local(): pl.pallas_call(functools.partial(first_kernel, devices, 'grid'), name='fi...  7.13 us
    pallas_call x1, Pallas kernels, local(): pl.pallas_call(functools.partial(second_kernel, devices, 'grid'), name='s...  6.55 us
    pallas_call x1, Pallas kernels, local(): pl.pallas_call(functools.partial(last_kernel, devices, 'grid'), name='las...  3.16 us
    pallas_call x1, Pallas kernels, local(): pl.pallas_call(functools.partial(shared_kernel, block_cols), name='shared...  1.88 us
    pallas_call x1, Pallas kernels, local(): pl.pallas_call(functools.partial(output_kernel, block_cols), name='second...  1.85 us

profile of v3, /device:TPU:1, one launch (start us, length us, event | category | flops | bytes accessed | tf_op | source)
XLA Modules:
  0.0 91.8 jit_solution(2682433027870092841)
XLA Ops:
  0.6 7.1 %first_cycle.1 = (f32[16,48,128]{2,1,0:T(8,128)S(1)}, f32[1024,128]{1,0:T(8,128)S(1)}, f32[1024,128]{1,0:T(8,128)S(1)}) custom-call(f32[1024,128]{1,0:T(8,128)} %bitcast.5, f32[8,128]{1,0:T(8,128)} %bitcast.3, f32[32]{0:T(128)} %rs.1, s32[16]{0:T(128)} %levels.7, s32[16]{0:T(128)} %assign_from.1, bf16[4,128,128]{2,1,0:T(8,128)(2,1)} %constant.6.clone.forward_hbm.forward, ...), custom_call_target="tpu_custom_call" | custom-call | tf_op jit(solution)/shard_map/first_cycle/pallas_call | solution.py:555
  7.8 0.0 copy-start.4
  7.8 0.0 copy-start.5
  7.8 0.0 copy-start.8
  7.8 19.1 %all_to_all.20.recv = f32[16,48,128]{2,1,0:T(8,128)S(1)} all-to-all(f32[16,48,128]{2,1,0:T(8,128)S(1)} %get-tuple-element.7), channel_id=1, replica_groups=mesh['groups'=2,'grid'=16] {'grid'}, dimensions={0} | all-to-all | bytes 786432 | tf_op jit(solution)/shard_map/all_to_all | solution.py:552
  26.9 0.0 copy-done.4
  26.9 0.0 copy-done.5
  26.9 0.0 copy-done.8
  26.9 1.9 %shared_rows.1 = f32[16,48,128]{2,1,0:T(8,128)S(1)} custom-call(f32[16,48,128]{2,1,0:T(8,128)S(1)} %all_to_all.20.recv, s32[16]{0:T(128)S(1)} %copy-done.4, s32[16]{0:T(128)S(1)} %copy-done.8, s32[16]{0:T(128)S(1)} %copy-done.5), custom_call_target="tpu_custom_call" | custom-call | tf_op jit(solution)/shard_map/shared_rows/pallas_call | solution.py:576
  28.8 0.0 copy-start
  28.8 0.0 copy-start.1
  28.8 0.0 copy-start.2
  28.8 15.5 %all_to_all.21.recv = f32[16,48,128]{2,1,0:T(8,128)S(1)} all-to-all(f32[16,48,128]{2,1,0:T(8,128)S(1)} %shared_rows.1), channel_id=1, replica_groups=mesh['groups'=2,'grid'=16] {'grid'}, dimensions={0} | all-to-all | bytes 786432 | tf_op jit(solution)/shard_map/all_to_all | solution.py:552
  44.3 0.0 copy-done
  44.4 0.0 copy-done.1
  44.4 0.0 copy-done.2
  44.4 6.5 %second_cycle.1 = f32[16,64,128]{2,1,0:T(8,128)S(1)} custom-call(f32[16,48,128]{2,1,0:T(8,128)S(1)} %all_to_all.21.recv, f32[1024,128]{1,0:T(8,128)S(1)} %get-tuple-element.8.kept, f32[1024,128]{1,0:T(8,128)S(1)} %get-tuple-element.9.speed, s32[16]{0:T(128)S(1)} %copy-done.4, s32[16]{0:T(128)S(1)} %copy-done.5, s32[16]{0:T(128)} %owner.1, ...), custom_call_target="tpu_custom_call" | custom-call | tf_op jit(solution)/shard_map/second_cycle/pallas_call | solution.py:585
  50.9 0.0 copy-start.7
  50.9 17.5 %all_to_all.22.recv = f32[16,64,128]{2,1,0:T(8,128)S(1)} all-to-all(f32[16,64,128]{2,1,0:T(8,128)S(1)} %second_cycle.1), channel_id=1, replica_groups=mesh['groups'=2,'grid'=16] {'grid'}, dimensions={0} | all-to-all | bytes 1048576 | tf_op jit(solution)/shard_map/all_to_all | solution.py:552
  68.5 0.0 copy-done.7
  68.5 1.9 %second_combined.1 = (f32[16,64,128]{2,1,0:T(8,128)S(1)}, f32[64,1280]{1,0:T(8,128)}) custom-call(f32[16,64,128]{2,1,0:T(8,128)S(1)} %all_to_all.22.recv, s32[16]{0:T(128)S(1)} %copy-done.4, s32[16]{0:T(128)S(1)} %copy-done.8, s32[16]{0:T(128)S(1)} %copy-done.5, s32[16]{0:T(128)S(1)} %copy-done.7), custom_call_target="tpu_custom_call" | custom-call | tf_op jit(solution)/shard_map/second_combined/pallas_call | solution.py:595
  70.3 18.4 %all_to_all.23.recv = f32[16,64,128]{2,1,0:T(8,128)S(1)} all-to-all(f32[16,64,128]{2,1,0:T(8,128)S(1)} %get-tuple-element.11), channel_id=1, replica_groups=mesh['groups'=2,'grid'=16] {'grid'}, dimensions={0} | all-to-all | bytes 1048576 | tf_op jit(solution)/shard_map/all_to_all | solution.py:552
  88.7 0.0 copy-done.9
  88.7 3.2 %last_step.1 = f32[1024,128]{1,0:T(8,128)} custom-call(f32[16,64,128]{2,1,0:T(8,128)S(1)} %all_to_all.23.recv, f32[8,128]{1,0:T(8,128)S(1)} %bitcast.4, f32[32]{0:T(128)S(1)} %copy-done.6, s32[16]{0:T(128)S(1)} %copy-done.4, s32[16]{0:T(128)S(1)} %copy-done.7, s32[16]{0:T(128)S(1)} %copy-done.9, bf16[4,128,128]{2,1,0:T(8,128)(2,1)S(1)} %copy-done.2, ...), custom_call_target="tpu_custom_call" | custom-call | tf_op jit(solution)/shard_map/last_step/pallas_call | solution.py:604
  (5 shorter events, 0.0 us)
Async XLA Ops:
  7.8 19.1 %copy-start.4 = (s32[16]{0:T(128)S(1)}, s32[16]{0:T(128)}, u32[]{:S(2)}) copy-start(s32[16]{0:T(128)} %levels.7) | copy-start | bytes 196
  7.8 19.1 %copy-start.5 = (s32[16]{0:T(128)S(1)}, s32[16]{0:T(128)}, u32[]{:S(2)}) copy-start(s32[16]{0:T(128)} %assign_from.1) | copy-start | bytes 196
  7.8 19.1 %copy-start.8 = (s32[16]{0:T(128)S(1)}, s32[16]{0:T(128)}, u32[]{:S(2)}) copy-start(s32[16]{0:T(128)} %coeffs.3) | copy-start | bytes 196
  28.8 15.6 %copy-start = (bf16[4,256,256]{2,1,0:T(8,128)(2,1)S(1)}, bf16[4,256,256]{2,1,0:T(8,128)(2,1)}, u32[]{:S(2)}) copy-start(bf16[4,256,256]{2,1,0:T(8,128)(2,1)} %constant.8.clone.stencil_hbm.stencil) | copy-start | bytes 1572868
  28.8 15.5 %copy-start.1 = (bf16[4,128,128]{2,1,0:T(8,128)(2,1)S(1)}, bf16[4,128,128]{2,1,0:T(8,128)(2,1)}, u32[]{:S(2)}) copy-start(bf16[4,128,128]{2,1,0:T(8,128)(2,1)} %constant.6.clone.forward_hbm.forward) | copy-start | bytes 393220
  28.8 15.5 %copy-start.2 = (bf16[4,128,128]{2,1,0:T(8,128)(2,1)S(1)}, bf16[4,128,128]{2,1,0:T(8,128)(2,1)}, u32[]{:S(2)}) copy-start(bf16[4,128,128]{2,1,0:T(8,128)(2,1)} %constant.7.clone.backward) | copy-start | bytes 393220
  50.9 17.5 %copy-start.7 = (s32[16]{0:T(128)S(1)}, s32[16]{0:T(128)}, u32[]{:S(2)}) copy-start(s32[16]{0:T(128)} %assign.5) | copy-start | bytes 196
  70.3 18.4 %copy-start.3 = (f32[1024]{0:T(1024)S(1)}, f32[1024]{0:T(1024)}, u32[]{:S(2)}) copy-start(f32[1024]{0:T(1024)} %param.12) | copy-start | bytes 12292
  70.3 18.4 %copy-start.6 = (f32[32]{0:T(128)S(1)}, f32[32]{0:T(128)}, u32[]{:S(2)}) copy-start(f32[32]{0:T(128)} %rs.1) | copy-start | bytes 388
  70.3 18.4 %copy-start.9 = (s32[16]{0:T(128)S(1)}, s32[16]{0:T(128)}, u32[]{:S(2)}) copy-start(s32[16]{0:T(128)} %owner.1) | copy-start | bytes 196
